TPU v7x, 32 devices: a whole 2x2x4 slice. The times are simulated.
32 devices in a mesh: gx: 2 (over y), gy: 4 (over z), lev: 4 (over x, core).
Axes of the slice: x: 2, y: 2, z: 4, core: 2. Of those that a mesh axis runs over, the one named last changes fastest.
Arguments:
- state: bfloat16 [256, 32, 8, 512], P('gx', 'gy', 'lev'), may hold values from -6 to 6
- obs_col: int32 [1024], P('gx'), may hold values from 0 to 127
- obs_row: int32 [1024], P('gx'), may hold values from 0 to 31
- foot_off: int32 [1024, 8], P('gx'), may hold values from 0 to 84
- obs_lev: int32 [1024], P('gx'), may hold values from 0 to 7
- obs_val: float32 [1024], P('gx'), may hold values from -6 to 6
- obs_err: float32 [1024], P('gx'), may hold values from 0.5 to 2
- loc: bfloat16 [256, 32, 512], P('gx', ('gy', 'lev')), may hold values from 0.099609375 to 1
Outputs:
- mean_out: float32 [256, 32, 8], P('gx', ('gy', 'lev'))
- anom_out: bfloat16 [256, 32, 8, 512], P('gx', ('gy', 'lev'))
All inputs are finite; a program needn't handle non-finite values.
Results may differ from a plain program's by a relative error of at most 0.009.
Values may be sent and summed in bfloat16 or wider, within the bound.
A program may use at most 64 MiB of HBM per device.

v0:
```python
import jax
import jax.numpy as jnp
from jax import lax
from jax.experimental import pallas as pl
from jax.experimental.pallas import tpu as pltpu
from jax.sharding import PartitionSpec as P

KF = 8
HW = 8
DY = 2
SUB = 8
LANES = 128
BLOCK = 64


def padded_2(array, sides, width):
    for axis, dim in sides:
        size, length = (lax.axis_size(axis), array.shape[dim])
        up = [(i, (i + 1) % size) for i in range(size)]
        down = [(j, i) for i, j in up]
        last = lax.slice_in_dim(array, length - width, length, axis=dim)
        first = lax.slice_in_dim(array, 0, width, axis=dim)
        before = lax.ppermute(last, axis, up)
        after = lax.ppermute(first, axis, down)
        array = jnp.concatenate([before, array, after], axis=dim)
    return array


def footprint_code(obs_col, obs_row, foot_off, ny_total):
    span = 2 * DY + 1
    shift_x = foot_off // span - HW
    shift_y = foot_off % span - DY
    x_ext = obs_col[:, None] + shift_x + HW
    y_glob = jnp.clip(obs_row[:, None] + shift_y, 0, ny_total - 1)
    return x_ext * ny_total + y_glob


def observe(block, y_start, foot_code, obs_lev, ny_total):
    padded = padded_2(block, (("gx", 0),), HW)
    ext_x, y_count, lev_count, members = padded.shape
    col_id = (
        jnp.arange(ext_x, dtype=jnp.int32)[:, None] * ny_total
        + y_start
        + jnp.arange(y_count, dtype=jnp.int32)[None, :]
    ).reshape(-1)
    n_obs = foot_code.shape[0]
    hit_count = jnp.zeros((n_obs, col_id.shape[0]), jnp.float32)
    for slot in range(foot_code.shape[1]):
        hit_count = hit_count + (foot_code[:, slot, None] == col_id[None, :]).astype(jnp.float32)
    level_hit = (obs_lev[:, None] == jnp.arange(lev_count, dtype=jnp.int32)[None, :]).astype(
        jnp.float32
    )
    select = (hit_count[:, :, None] * level_hit[:, None, :]).reshape(n_obs, -1).astype(jnp.bfloat16)
    return jnp.dot(select, padded.reshape(-1, members), preferred_element_type=jnp.float32)


def relay(state):
    return lax.all_to_all(state, "lev", split_axis=1, concat_axis=2, tiled=True)


def lane_cast(value, k):
    return jnp.broadcast_to(value[:, k : k + 1], value.shape)


def row_cast(value, i):
    return jnp.broadcast_to(value[i : i + 1, :], value.shape)


def f32_dot(a, b, dims):
    return lax.dot_general(
        a, b, (dims, ((), ())), precision=lax.Precision.HIGHEST, preferred_element_type=jnp.float32
    )


def factor_block(w_ref, x_ref, root_err):
    rows = w_ref.shape[0]
    groups = rows // SUB
    w = [w_ref[SUB * g : SUB * (g + 1), :] for g in range(groups)]
    x = [x_ref[SUB * g : SUB * (g + 1), :] for g in range(groups)]
    sub_id = lax.broadcasted_iota(jnp.int32, (SUB, LANES), 0)
    for g in range(groups):
        col = {h: [lane_cast(w[h], SUB * g + m) for m in range(SUB)] for h in range(g, groups)}
        s = {(i, m): row_cast(col[g][m], i) for m in range(SUB) for i in range(m, SUB)}
        wr = [row_cast(w[g], i) for i in range(SUB)]
        xr = [row_cast(x[g], i) for i in range(SUB)]
        inv = []
        for k in range(SUB):
            pivot = s[k, k]
            inv_k = lax.rsqrt(pivot)
            inv.append(inv_k)
            minv_k = 1.0 / (pivot * inv_k + row_cast(root_err[g], k))
            for i in range(k + 1, SUB):
                s[i, k] = s[i, k] * inv_k
            for m in range(k + 1, SUB):
                for i in range(m, SUB):
                    s[i, m] = s[i, m] - s[i, k] * s[m, k]
            wr[k] = wr[k] * inv_k
            xr[k] = xr[k] * minv_k
            for i in range(k + 1, SUB):
                wr[i] = wr[i] - s[i, k] * wr[k]
                xr[i] = xr[i] - s[i, k] * xr[k]
        w_new, x_new = wr[0], xr[0]
        for k in range(1, SUB):
            w_new = jnp.where(sub_id == k, wr[k], w_new)
            x_new = jnp.where(sub_id == k, xr[k], x_new)
        w[g], x[g] = w_new, x_new
        for k in reversed(range(SUB)):
            wr[k] = wr[k] * inv[k]
            xr[k] = xr[k] * inv[k]
            for i in range(k):
                wr[i] = wr[i] - s[k, i] * wr[k]
                xr[i] = xr[i] - s[k, i] * xr[k]
        for h in range(g + 1, groups):
            for m in range(SUB):
                w[h] = w[h] - col[h][m] * wr[m]
                x[h] = x[h] - col[h][m] * xr[m]
    for g in range(groups):
        w_ref[SUB * g : SUB * (g + 1), :] = w[g]
        x_ref[SUB * g : SUB * (g + 1), :] = x[g]


def weights_kernel(hx_ref, val_ref, err_ref, z_ref, w_out_ref, y_ref, a_ref, s_ref, root_ref, w_ref, x_ref, inv_ref, low_ref):
    n, members = hx_ref.shape
    blocks = n // BLOCK
    hx = hx_ref[...]
    hbar = jnp.mean(hx, axis=1, keepdims=True)
    yanom = hx - hbar
    y_ref[...] = yanom.astype(jnp.bfloat16)
    s_ref[:, :members] = yanom
    s_ref[:, members:] = jnp.broadcast_to(val_ref[...] - hbar, (n, LANES))
    root_ref[...] = jnp.broadcast_to(jnp.sqrt(err_ref[...]), (n, LANES))
    same = lax.broadcasted_iota(jnp.int32, (n, n), 0) == lax.broadcasted_iota(jnp.int32, (n, n), 1)
    a_ref[...] = f32_dot(yanom, yanom, ((1,), (1,))) / (members - 1) + jnp.where(same, err_ref[...], 0.0)
    eye_w = lax.broadcasted_iota(jnp.int32, (BLOCK, LANES), 0) + BLOCK == lax.broadcasted_iota(jnp.int32, (BLOCK, LANES), 1)
    eye_x = lax.broadcasted_iota(jnp.int32, (BLOCK, LANES), 0) == lax.broadcasted_iota(jnp.int32, (BLOCK, LANES), 1)

    def load_block(at):
        w_ref[...] = jnp.where(eye_w, 1.0, 0.0)
        w_ref[:, :BLOCK] = a_ref[at : at + BLOCK, at : at + BLOCK]
        x_ref[...] = jnp.where(eye_x, 1.0, 0.0)

    load_block(0)

    def step(k, carry):
        base = pl.multiple_of(k * BLOCK, BLOCK)
        root_err = [root_ref[pl.ds(base + SUB * g, SUB), :] for g in range(BLOCK // SUB)]
        factor_block(w_ref, x_ref, root_err)
        for kk in range(blocks):

            @pl.when(k == kk)
            def _():
                at, end = kk * BLOCK, (kk + 1) * BLOCK
                l_inv = w_ref[:, BLOCK:]
                m_inv = x_ref[:, :BLOCK]
                inv_ref[kk] = l_inv
                s_ref[at:end, :members] = f32_dot(m_inv, s_ref[at:end, :members], ((1,), (0,)))
                s_ref[at:end, members:] = f32_dot(l_inv, s_ref[at:end, members:], ((1,), (0,)))
                if end < n:
                    left = end // LANES * LANES
                    panel = f32_dot(a_ref[left:, at:end], l_inv, ((1,), (1,)))
                    below = panel[end - left :]
                    low_ref[kk, end:, :] = below
                    a_ref[end:, left:] = a_ref[end:, left:] - f32_dot(below, panel, ((1,), (1,)))
                    load_block(end)
                    s_ref[end:, :] = s_ref[end:, :] - f32_dot(below, s_ref[at:end, :], ((1,), (0,)))

        return carry

    lax.fori_loop(0, blocks, step, 0)
    for kk in reversed(range(blocks)):
        at, end = kk * BLOCK, (kk + 1) * BLOCK
        right = s_ref[at:end, :]
        if end < n:
            right = right - f32_dot(low_ref[kk, end:, :], s_ref[end:, :], ((0,), (0,)))
        s_ref[at:end, :] = f32_dot(inv_ref[kk], right, ((0,), (0,)))
    z_ref[...] = s_ref[:, :members].astype(jnp.bfloat16)
    w_out_ref[...] = s_ref[:, members:]


def weights(hx, values, errors):
    n, members = hx.shape
    return pl.pallas_call(
        weights_kernel,
        name="weights",
        out_shape=(
            jax.ShapeDtypeStruct((n, members), jnp.bfloat16),
            jax.ShapeDtypeStruct((n, LANES), jnp.float32),
            jax.ShapeDtypeStruct((n, members), jnp.bfloat16),
        ),
        in_specs=[pl.BlockSpec(memory_space=pltpu.VMEM)] * 3,
        out_specs=tuple([pl.BlockSpec(memory_space=pltpu.VMEM)] * 3),
        scratch_shapes=[
            pltpu.VMEM((n, n), jnp.float32),
            pltpu.VMEM((n, members + LANES), jnp.float32),
            pltpu.VMEM((n, LANES), jnp.float32),
            pltpu.VMEM((BLOCK, LANES), jnp.float32),
            pltpu.VMEM((BLOCK, LANES), jnp.float32),
            pltpu.VMEM((n // BLOCK, BLOCK, BLOCK), jnp.float32),
            pltpu.VMEM((n // BLOCK, n, BLOCK), jnp.float32),
        ],
        compiler_params=pltpu.CompilerParams(vmem_limit_bytes=48 * 1024 * 1024),
    )(hx, values[:, None], errors[:, None])


def analyse(block, weight, hx_sum, values, errors):
    members = block.shape[-1]
    zmat, wcol, ybf = weights(hx_sum, values, errors)
    wvec = wcol[:, 0]
    xbar = jnp.mean(block, axis=-1, dtype=jnp.float32)
    anom = (block.astype(jnp.float32) - xbar[..., None]).astype(jnp.bfloat16)
    flat = anom.reshape(-1, members)
    cross = jnp.dot(flat, ybf.T, preferred_element_type=jnp.float32) / (
        members - 1
    )
    n_obs = hx_sum.shape[0]
    gain = (
        cross.reshape(block.shape[:-1] + (n_obs,)) * weight[:, :, None, :].astype(jnp.float32)
    ).astype(jnp.bfloat16)
    mean_part = xbar + jnp.sum(gain.astype(jnp.float32) * wvec, axis=-1)
    update = jnp.dot(gain.reshape(-1, n_obs), zmat, preferred_element_type=jnp.float32)
    anom_part = (flat.astype(jnp.float32) - update).astype(jnp.bfloat16).reshape(block.shape)
    return (mean_part, anom_part)


def local(state, obs_col, obs_row, foot_off, obs_lev, obs_val, obs_err, loc):
    level_groups = lax.axis_size("lev")
    ny_total = loc.shape[1] * lax.axis_size("gy") * level_groups
    foot_code = footprint_code(obs_col, obs_row, foot_off, ny_total)
    y_block = loc.shape[1]
    relaid = relay(state)
    y_start = (lax.axis_index("gy") * level_groups + lax.axis_index("lev")) * y_block
    partial_sum = observe(relaid, y_start, foot_code, obs_lev, ny_total)
    hx_sum = lax.psum(partial_sum, ("gy", "lev")) / KF
    return analyse(relaid, loc, hx_sum, obs_val, obs_err)


def solution(mesh):
    return jax.shard_map(
        local,
        mesh=mesh,
        in_specs=(
            P("gx", "gy", "lev", None),
            P("gx"),
            P("gx"),
            P("gx", None),
            P("gx"),
            P("gx"),
            P("gx"),
            P("gx", ("gy", "lev"), None),
        ),
        out_specs=(P("gx", ("gy", "lev"), None), P("gx", ("gy", "lev"), None, None)),
        check_vma=False,
    )
```

profile of v0, /device:TPU:0, one launch (start us, length us, event | category | flops | bytes accessed | tf_op | source)
XLA Modules:
  0.0 210.5 jit_solution(8941541582516567096)
XLA Ops:
  7.2 4.3 %copy.23 = bf16[128,8,2,512]{3,2,0,1:T(2,128)(2,1)} copy(bf16[128,8,2,512]{3,2,1,0:T(2,128)(2,1)} %param.8) | data formatting | bytes 4194304 | tf_op args[0]
  11.5 0.0 copy-start.3
  11.5 0.0 copy-start.4
  11.5 4.4 %all-to-all-start = ((bf16[128,8,2,512]{3,2,0,1:T(2,128)(2,1)}), bf16[128,8,2,512]{3,2,0,1:T(2,128)(2,1)S(1)}, u32[]{:S(2)}, u32[]{:S(2)}) async-start(bf16[128,8,2,512]{3,2,0,1:T(2,128)(2,1)} %copy.23), calls=%async_computation | async-start | bytes 4194304 | tf_op jit(solution)/shard_map/all_to_all | solution.py:58
  15.9 0.0 all-reduce.2.cloned.1.call-start
  15.9 0.1 iota_add_fusion
  16.0 0.1 add.132
  16.1 0.0 copy-done.3
  16.1 0.1 copy.26.val_ref
  16.3 0.0 copy-done.4
  16.3 0.1 copy.27.err_ref
  16.4 0.0 copy-done.1
  16.5 2.6 %mul.76 = f32[128,2,8,512]{3,2,1,0:T(8,128)} broadcast(bf16[128,2,512]{2,1,0:T(2,128)(2,1)S(1)} %copy-done.1), dimensions={0,1,3} | broadcast | bytes 4456448 | tf_op jit(solution)/shard_map/mul | solution.py:217
  19.1 5.5 %copy.28 = f32[2048,512]{0,1:T(8,128)} copy(f32[2048,512]{1,0:T(8,128)} %bitcast.31) | data formatting | bytes 8388608 | tf_op jit(solution)/shard_map/mul | solution.py:217
  24.5 0.0 copy-done.2
  24.5 0.0 copy-done.5
  24.5 0.0 copy-done.6
  24.6 0.5 convert_add_fusion
  25.1 0.0 copy-start.7
  25.1 16.5 %all-to-all-done = bf16[128,8,2,512]{3,2,0,1:T(2,128)(2,1)S(1)} async-done(((bf16[128,8,2,512]{3,2,0,1:T(2,128)(2,1)}), bf16[128,8,2,512]{3,2,0,1:T(2,128)(2,1)S(1)}, u32[]{:S(2)}, u32[]{:S(2)}) %all-to-all-start) | async-done | bytes 2097184 | tf_op jit(solution)/shard_map/all_to_all | solution.py:58
  41.6 4.7 %fusion.15 = (f32[128,2,4,2,512]{4,3,2,1,0:T(2,128)}, bf16[128,2,4,2,512]{4,3,2,1,0:T(2,128)(2,1)S(1)}) fusion(bf16[128,8,2,512]{3,2,0,1:T(2,128)(2,1)S(1)} %all-to-all-done), kind=kLoop, calls=%fused_computation.33 | loop fusion | flops 1048576 | bytes 8388608 | tf_op jit(solution)/shard_map/convert_element_type | solution.py:209
  46.3 1.3 copy-done
  47.6 0.2 fusion.16
  47.8 0.7 slice.72
  48.6 2.3 %collective-permute-start = (bf16[8,2,8,512]{3,2,1,0:T(8,128)(2,1)}, bf16[8,2,8,512]{3,2,1,0:T(8,128)(2,1)S(1)}, u32[]{:S(2)}, u32[]{:S(2)}) collective-permute-start(bf16[8,2,8,512]{3,2,1,0:T(8,128)(2,1)} %slice.72), channel_id=1, source_target_pairs={{0,16},{16,0},{1,17},{17,1},{2,18},{18,2},{3,19},{19,3},{4,20},{20... | collective-permute-start | bytes 393224 | tf_op jit(solution)/shard_map/ppermute | solution.py:23
  50.9 0.7 slice.74
  51.6 0.0 collective-permute-start.1
  51.6 0.0 copy-done.7
  51.6 4.1 %all_to_all.16 = bf16[128,2,8,512]{3,2,1,0:T(8,128)(2,1)} reshape(bf16[128,2,4,2,512]{4,3,2,1,0:T(2,128)(2,1)} %copy-done) | data formatting | bytes 4194304 | tf_op jit(solution)/shard_map/all_to_all | solution.py:58
  55.8 0.0 collective-permute-done
  55.8 1.3 collective-permute-done.1
  57.1 1.9 pad_maximum_fusion
  59.0 2.4 %fusion.1 = f32[512,512]{1,0:T(8,128)} fusion(bf16[2304,512]{1,0:T(8,128)(2,1)S(1)} %bitcast.32, f32[512,8]{0,1:T(8,128)S(1)} %fusion.14, f32[512,288]{0,1:T(8,128)S(1)} %convert_add_fusion), kind=kOutput, calls=%fused_computation.6 | convolution fusion | flops 1210318848 | bytes 4014080 | tf_op jit(solution)/shard_map/dot_general | solution.py:54
  61.4 0.0 all-reduce.2.cloned.1.call-update
  61.4 2.1 %convert_reduce_fusion = f32[128,2,4,2]{3,2,1,0:T(4,128)S(1)} fusion(bf16[128,4,2,2,512]{4,3,0,2,1:T(2,128)(2,1)S(1)} %bitcast.30), kind=kLoop, calls=%fused_computation.11 | loop fusion | flops 2095104 | bytes 2105344 | tf_op jit(solution)/shard_map/reduce_sum | solution.py:209
  63.5 0.1 broadcast_multiply_fusion.1
  63.7 0.4 div.31
  64.1 0.2 copy.25
  64.4 6.2 %reshape.340 = f32[2048,512]{1,0:T(8,128)} reshape(f32[128,2,4,2,512]{4,3,2,1,0:T(2,128)} %get-tuple-element.10) | data formatting | bytes 8388608 | tf_op jit(solution)/shard_map/convert_element_type | solution.py:209
  70.5 85.5 %all-reduce.2.cloned.1.call-done = f32[512,512]{1,0:T(8,128)} async-done(((f32[512,512]{1,0:T(8,128)}), f32[512,512]{1,0:T(8,128)}) %all-reduce.2.cloned.1.call-update) | async-done | bytes 1048592 | tf_op jit(solution)/shard_map/psum | solution.py:233
  156.0 1.3 broadcast_multiply_fusion.hx_ref
  157.3 35.5 %weights.1 = (bf16[512,512]{1,0:T(8,128)(2,1)S(1)}, f32[512,128]{1,0:T(8,128)S(1)}, bf16[512,512]{1,0:T(8,128)(2,1)S(1)}) custom-call(f32[512,512]{1,0:T(8,128)S(1)} %broadcast_multiply_fusion.hx_ref, f32[512,1]{1,0:T(8,128)S(1)} %copy.26.val_ref, f32[512,1]{1,0:T(8,128)S(1)} %copy.27.err_ref), custom_call_target="tpu_custom_call" | custom-call | tf_op jit(solution)/shard_map/weights/pallas_call | solution.py:182
  192.8 0.1 slice_reduce_fusion
  193.0 5.0 %multiply_reduce_fusion = (f32[2048]{0:T(1024)S(1)}, bf16[2048,512]{0,1:T(8,128)(2,1)S(1)}) fusion(f32[512]{0:T(512)S(1)} %slice_reduce_fusion, f32[2048,512]{0,1:T(8,128)} %copy.28, bf16[512,512]{1,0:T(8,128)(2,1)S(1)} %get-tuple-element.5, f32[2048,512]{1,0:T(8,128)} %reshape.340, f32[2048]{0:T(1024)S(1)} %div.31), kind=kOutput, calls=%fused_computation.2 | convolution fusion | flops 1082128384 | bytes 11028480 | tf_op jit(solution)/shard_map/dot_general | solution.py:212
  197.9 0.2 reduce_sum.22
  198.2 0.1 copy.29
  198.2 4.8 %subtract_convert_fusion = bf16[2048,512]{1,0:T(8,128)(2,1)} fusion(bf16[2048,512]{0,1:T(8,128)(2,1)S(1)} %get-tuple-element.23, bf16[512,512]{1,0:T(8,128)(2,1)S(1)} %get-tuple-element.7, f32[2048,512]{1,0:T(8,128)} %reshape.340, f32[2048]{0:T(1024)S(1)} %div.31), kind=kOutput, calls=%fused_computation.1 | convolution fusion | flops 1078984704 | bytes 8921088 | tf_op jit(solution)/shard_map/dot_general | solution.py:220
  203.1 0.6 add.140
  (9 shorter events, 0.1 us)
Async XLA Ops:
  11.5 4.6 %copy-start.3 = (f32[512]{0:T(512)S(1)}, f32[512]{0:T(512)}, u32[]{:S(2)}) copy-start(f32[512]{0:T(512)} %param.13) | copy-start | bytes 6148
  11.5 4.8 %copy-start.4 = (f32[512]{0:T(512)S(1)}, f32[512]{0:T(512)}, u32[]{:S(2)}) copy-start(f32[512]{0:T(512)} %param.14) | copy-start | bytes 6148
  11.5 4.9 %copy-start.1 = (bf16[128,2,512]{2,1,0:T(2,128)(2,1)S(1)}, bf16[128,2,512]{2,1,0:T(2,128)(2,1)}, u32[]{:S(2)}) copy-start(bf16[128,2,512]{2,1,0:T(2,128)(2,1)} %param.15) | copy-start | bytes 786436
  11.5 30.0 %all-to-all-start = ((bf16[128,8,2,512]{3,2,0,1:T(2,128)(2,1)}), bf16[128,8,2,512]{3,2,0,1:T(2,128)(2,1)S(1)}, u32[]{:S(2)}, u32[]{:S(2)}) async-start(bf16[128,8,2,512]{3,2,0,1:T(2,128)(2,1)} %copy.23), calls=%async_computation | async-start | bytes 4194304 | tf_op jit(solution)/shard_map/all_to_all | solution.py:58
  15.9 140.1 %all-reduce.2.cloned.1.call-start = ((), (), s32[]{:S(2)}) async-start(), calls=%async_computation.1 | async-start | bytes 2097152 | tf_op jit(solution)/shard_map/psum | solution.py:233
  19.1 5.5 %copy-start.2 = (s32[512,8]{0,1:T(8,128)S(1)}, s32[512,8]{0,1:T(8,128)}, u32[]{:S(2)}) copy-start(s32[512,8]{0,1:T(8,128)} %param.11) | copy-start | bytes 49156
  19.1 5.5 %copy-start.5 = (s32[512]{0:T(512)S(1)}, s32[512]{0:T(512)}, u32[]{:S(2)}) copy-start(s32[512]{0:T(512)} %param.10) | copy-start | bytes 6148
  19.1 5.5 %copy-start.6 = (s32[512]{0:T(512)S(1)}, s32[512]{0:T(512)}, u32[]{:S(2)}) copy-start(s32[512]{0:T(512)} %param.9) | copy-start | bytes 6148
  25.1 26.5 %copy-start.7 = (s32[512]{0:T(512)S(1)}, s32[512]{0:T(512)}, u32[]{:S(2)}) copy-start(s32[512]{0:T(512)} %param.12) | copy-start | bytes 6148
  46.3 1.3 copy-start
  48.6 7.2 %collective-permute-start = (bf16[8,2,8,512]{3,2,1,0:T(8,128)(2,1)}, bf16[8,2,8,512]{3,2,1,0:T(8,128)(2,1)S(1)}, u32[]{:S(2)}, u32[]{:S(2)}) collective-permute-start(bf16[8,2,8,512]{3,2,1,0:T(8,128)(2,1)} %slice.72), channel_id=1, source_target_pairs={{0,16},{16,0},{1,17},{17,1},{2,18},{18,2},{3,19},{19,3},{4,20},{20... | collective-permute-start | bytes 393224 | tf_op jit(solution)/shard_map/ppermute | solution.py:23
  51.6 5.5 %collective-permute-start.1 = (bf16[8,2,8,512]{3,2,1,0:T(8,128)(2,1)}, bf16[8,2,8,512]{3,2,1,0:T(8,128)(2,1)S(1)}, u32[]{:S(2)}, u32[]{:S(2)}) collective-permute-start(bf16[8,2,8,512]{3,2,1,0:T(8,128)(2,1)} %slice.74), channel_id=1, source_target_pairs={{16,0},{0,16},{17,1},{1,17},{18,2},{2,18},{19,3},{3,19},{20,4},{4,... | collective-permute-start | bytes 393224 | tf_op jit(solution)/shard_map/ppermute | solution.py:24
Sparse Core Ops, SparseCore 0:
  61.5 94.4 all-reduce.1
where the time goes:
time: 211 us
  waiting for transfers between devices  103 us (49%)
  Pallas kernels  35.5 us (17%)
  local copies, waits for them, and re-layouts  27.2 us (13%)
  between operations  14.2 us (7%)
  matrix products  12.2 us (6%)
  other arithmetic  11.4 us (5%)
  starting transfers between devices  6.7 us (3%)
    psum x1, waiting for transfers between devices, local(): hx_sum = lax.psum(partial_sum, ('gy', 'lev')) / KF  85.5 us
    pallas_call x1, Pallas kernels, weights(): pl.pallas_call(weights_kernel, name='weights', out_shape=(jax.ShapeDtypeS...  35.5 us
    all_to_all x1, waiting for transfers between devices, relay(): return lax.all_to_all(state, 'lev', split_axis=1, concat_axis=2, tiled=True)  16.5 us
    mul x2, local copies, waits for them, and re-layouts, analyse(): cross.reshape(block.shape[:-1] + (n_obs,))  8.04 us
    convert_element_type x1, local copies, waits for them, and re-layouts, analyse(): xbar = jnp.mean(block, axis=-1, dtype=jnp.float32)  6.15 us
    unnamed x17, local copies, waits for them, and re-layouts  5.7 us
    dot_general x1, matrix products, analyse(): jnp.dot(flat, ybf.T, preferred_element_type=jnp.float32) / (members - 1)  4.97 us
    dot_general x1, matrix products, analyse(): jnp.dot(gain.reshape(-1, n_obs), zmat, preferred_element_type=jnp.float32)  4.82 us
  transfers between devices with their start and end apart: 4, of which 3 were waited for; matrix products, arithmetic and copies ran while one was open for 9% of the time, Pallas kernels for 0%

commit v1 on v0

--- a/solution.py
+++ b/solution.py
@@ -1,3 +1,5 @@
+import functools
+
 import jax
 import jax.numpy as jnp
 from jax import lax
@@ -11,51 +13,19 @@
 SUB = 8
 LANES = 128
 BLOCK = 64
-
-
-def padded_2(array, sides, width):
-    for axis, dim in sides:
-        size, length = (lax.axis_size(axis), array.shape[dim])
-        up = [(i, (i + 1) % size) for i in range(size)]
-        down = [(j, i) for i, j in up]
-        last = lax.slice_in_dim(array, length - width, length, axis=dim)
-        first = lax.slice_in_dim(array, 0, width, axis=dim)
-        before = lax.ppermute(last, axis, up)
-        after = lax.ppermute(first, axis, down)
-        array = jnp.concatenate([before, array, after], axis=dim)
-    return array
-
-
-def footprint_code(obs_col, obs_row, foot_off, ny_total):
+MESH = pl.DeviceIdType.MESH
+
+
+def footprint_code(obs_col, obs_row, foot_off, obs_lev, shape, ny_total, y_start, lev_start):
+    y_count, lev_count = shape
     span = 2 * DY + 1
     shift_x = foot_off // span - HW
     shift_y = foot_off % span - DY
     x_ext = obs_col[:, None] + shift_x + HW
-    y_glob = jnp.clip(obs_row[:, None] + shift_y, 0, ny_total - 1)
-    return x_ext * ny_total + y_glob
-
-
-def observe(block, y_start, foot_code, obs_lev, ny_total):
-    padded = padded_2(block, (("gx", 0),), HW)
-    ext_x, y_count, lev_count, members = padded.shape
-    col_id = (
-        jnp.arange(ext_x, dtype=jnp.int32)[:, None] * ny_total
-        + y_start
-        + jnp.arange(y_count, dtype=jnp.int32)[None, :]
-    ).reshape(-1)
-    n_obs = foot_code.shape[0]
-    hit_count = jnp.zeros((n_obs, col_id.shape[0]), jnp.float32)
-    for slot in range(foot_code.shape[1]):
-        hit_count = hit_count + (foot_code[:, slot, None] == col_id[None, :]).astype(jnp.float32)
-    level_hit = (obs_lev[:, None] == jnp.arange(lev_count, dtype=jnp.int32)[None, :]).astype(
-        jnp.float32
-    )
-    select = (hit_count[:, :, None] * level_hit[:, None, :]).reshape(n_obs, -1).astype(jnp.bfloat16)
-    return jnp.dot(select, padded.reshape(-1, members), preferred_element_type=jnp.float32)
-
-
-def relay(state):
-    return lax.all_to_all(state, "lev", split_axis=1, concat_axis=2, tiled=True)
+    y_here = jnp.clip(obs_row[:, None] + shift_y, 0, ny_total - 1) - y_start
+    lev_here = obs_lev[:, None] - lev_start
+    inside = (y_here >= 0) & (y_here < y_count) & (lev_here >= 0) & (lev_here < lev_count)
+    return jnp.where(inside, (x_ext * y_count + y_here) * lev_count + lev_here, -1)
 
 
 def lane_cast(value, k):
@@ -119,18 +89,14 @@
         x_ref[SUB * g : SUB * (g + 1), :] = x[g]
 
 
-def weights_kernel(hx_ref, val_ref, err_ref, z_ref, w_out_ref, y_ref, a_ref, s_ref, root_ref, w_ref, x_ref, inv_ref, low_ref):
-    n, members = hx_ref.shape
+def solve_weights(err_ref, z_ref, w_out_ref, y_ref, a_ref, s_ref, root_ref, w_ref, x_ref, inv_ref, low_ref):
+    n, members = y_ref.shape
     blocks = n // BLOCK
-    hx = hx_ref[...]
-    hbar = jnp.mean(hx, axis=1, keepdims=True)
-    yanom = hx - hbar
-    y_ref[...] = yanom.astype(jnp.bfloat16)
-    s_ref[:, :members] = yanom
-    s_ref[:, members:] = jnp.broadcast_to(val_ref[...] - hbar, (n, LANES))
+    ybf = s_ref[:, :members].astype(jnp.bfloat16)
+    y_ref[...] = ybf
     root_ref[...] = jnp.broadcast_to(jnp.sqrt(err_ref[...]), (n, LANES))
     same = lax.broadcasted_iota(jnp.int32, (n, n), 0) == lax.broadcasted_iota(jnp.int32, (n, n), 1)
-    a_ref[...] = f32_dot(yanom, yanom, ((1,), (1,))) / (members - 1) + jnp.where(same, err_ref[...], 0.0)
+    a_ref[...] = lax.dot_general(ybf, ybf, (((1,), (1,)), ((), ())), preferred_element_type=jnp.float32) / (members - 1) + jnp.where(same, err_ref[...], 0.0)
     eye_w = lax.broadcasted_iota(jnp.int32, (BLOCK, LANES), 0) + BLOCK == lax.broadcasted_iota(jnp.int32, (BLOCK, LANES), 1)
     eye_x = lax.broadcasted_iota(jnp.int32, (BLOCK, LANES), 0) == lax.broadcasted_iota(jnp.int32, (BLOCK, LANES), 1)
 
@@ -177,19 +143,164 @@
     w_out_ref[...] = s_ref[:, members:]
 
 
-def weights(hx, values, errors):
-    n, members = hx.shape
+def analysis_weights_kernel(
+    axes, code_ref, state_ref, raw_ref, val_ref, err_ref, z_ref, w_out_ref, y_ref, relaid_ref,
+    acc_ref, before_ref, after_ref, zin_ref, ys_ref, hb_ref, half_refs,
+    a_ref, s_ref, root_ref, w_ref, x_ref, inv_ref, low_ref, send_sem, recv_sem, own_sem,
+):
+    gxs, gys, levs = axes
+    gx, gy, lev = lax.axis_index("gx"), lax.axis_index("gy"), lax.axis_index("lev")
+    n, members = acc_ref.shape
+    edge = before_ref.shape[0]
+    inner = state_ref.shape[0]
+    right, left = lax.rem(gx + 1, gxs), lax.rem(gx + gxs - 1, gxs)
+    levels = [(lax.rem(lev + d, levs)) for d in range(1, levs)]
+    lats = [(lax.rem(gy + d, gys)) for d in range(1, gys)]
+    barrier = pltpu.get_barrier_semaphore()
+    peers = [{"gx": right}, {"gx": left}] + [{"lev": v} for v in levels] + [{"gy": v} for v in lats]
+    for peer in peers:
+        pl.semaphore_signal(barrier, inc=1, device_id=peer, device_id_type=MESH)
+    pl.semaphore_wait(barrier, len(peers))
+    count = [0]
+
+    def remote(src, dst, peer):
+        i = count[0]
+        count[0] += 1
+        return pltpu.make_async_remote_copy(
+            src_ref=src, dst_ref=dst, send_sem=send_sem.at[i], recv_sem=recv_sem.at[i],
+            device_id=peer, device_id_type=MESH,
+        )
+
+    halo = [
+        remote(state_ref.at[inner - edge : inner], before_ref, {"gx": right}),
+        remote(state_ref.at[0:edge], after_ref, {"gx": left}),
+    ]
+    for copy in halo:
+        copy.start()
+    y_block = relaid_ref.shape[2]
+    own = pltpu.make_async_copy(raw_ref.at[:, pl.ds(lev * y_block, y_block)], relaid_ref.at[lev], own_sem.at[0])
+    own.start()
+
+    def chosen(base, width):
+        spot = lax.broadcasted_iota(jnp.int32, (n, width), 1) + base
+        hits = jnp.zeros((n, width), jnp.float32)
+        for slot in range(KF):
+            hits = hits + jnp.where(code_ref[:, slot : slot + 1] == spot, 1.0, 0.0)
+        return hits.astype(jnp.bfloat16)
+
+    acc_ref[...] = jnp.zeros_like(acc_ref)
+    width = 256
+
+    def pick(i, carry):
+        at = pl.multiple_of(i * width, width)
+        acc_ref[...] += jnp.dot(
+            chosen(edge + at, width), state_ref[pl.ds(at, width), :], preferred_element_type=jnp.float32
+        )
+        return carry
+
+    lax.fori_loop(0, inner // width, pick, 0)
+    sel_before, sel_after = chosen(0, edge), chosen(edge + inner, edge)
+    for copy in halo:
+        copy.wait()
+    acc_ref[...] += jnp.dot(sel_before, before_ref[...], preferred_element_type=jnp.float32) + jnp.dot(
+        sel_after, after_ref[...], preferred_element_type=jnp.float32
+    )
+    base, size = 0, n
+    bits = levs.bit_length() - 1
+    bases = []
+    for b in range(bits):
+        size //= 2
+        bit = lax.rem(lev // (1 << b), 2)
+        partner = lev + (1 - 2 * bit) * (1 << b)
+        keep, give = base + bit * size, base + (1 - bit) * size
+        copy = remote(acc_ref.at[pl.ds(pl.multiple_of(give, 8), size)], half_refs[b], {"lev": partner})
+        copy.start()
+        copy.wait()
+        rows = pl.ds(pl.multiple_of(keep, 8), size)
+        acc_ref[rows, :] = acc_ref[rows, :] + half_refs[b][...]
+        base = keep
+        bases.append((base, size, partner))
+    part = n // (levs * gys)
+    copies = []
+    for d, lat in enumerate(lats):
+        copies.append(
+            remote(acc_ref.at[pl.ds(pl.multiple_of(base + lat * part, 8), part)], zin_ref.at[d], {"gy": lat})
+        )
+    for copy in copies:
+        copy.start()
+    for copy in copies:
+        copy.wait()
+    mine = base + gy * part
+    total = acc_ref[pl.ds(pl.multiple_of(mine, 8), part), :]
+    for d in range(gys - 1):
+        total = total + zin_ref[d]
+    hx = total / KF
+    hbar = jnp.mean(hx, axis=1, keepdims=True)
+    chunk = base // part + gy
+    ys_ref[chunk] = (hx - hbar).astype(jnp.bfloat16)
+    hb_ref[chunk] = jnp.broadcast_to(hbar, (part, LANES))
+    copies = []
+    for lat in lats:
+        copies.append(remote(ys_ref.at[chunk], ys_ref.at[chunk], {"gy": lat}))
+        copies.append(remote(hb_ref.at[chunk], hb_ref.at[chunk], {"gy": lat}))
+    for copy in copies:
+        copy.start()
+    for copy in copies:
+        copy.wait()
+    for start, size, partner in reversed(bases):
+        span = pl.ds(start // part, size // part)
+        copies = [
+            remote(ys_ref.at[span], ys_ref.at[span], {"lev": partner}),
+            remote(hb_ref.at[span], hb_ref.at[span], {"lev": partner}),
+        ]
+        for copy in copies:
+            copy.start()
+        for copy in copies:
+            copy.wait()
+    copies = [
+        remote(raw_ref.at[:, pl.ds(v * y_block, y_block)], relaid_ref.at[lev], {"lev": v}) for v in levels
+    ]
+    for copy in copies:
+        copy.start()
+    for c in range(levs * gys):
+        s_ref[c * part : (c + 1) * part, :members] = ys_ref[c].astype(jnp.float32)
+        s_ref[c * part : (c + 1) * part, members:] = val_ref[c * part : (c + 1) * part, :] - hb_ref[c]
+    solve_weights(err_ref, z_ref, w_out_ref, y_ref, a_ref, s_ref, root_ref, w_ref, x_ref, inv_ref, low_ref)
+    for copy in copies:
+        copy.wait()
+    own.wait()
+
+
+def analysis_weights(state, code, values, errors):
+    axes = tuple(lax.axis_size(name) for name in ("gx", "gy", "lev"))
+    gxs, gys, levs = axes
+    x_count, y_count, lev_count, members = state.shape
+    n = values.shape[0]
+    edge = HW * y_count * lev_count
+    part = n // (gys * levs)
+    bits = levs.bit_length() - 1
+    copies = 2 + bits + (gys - 1) + 2 * (gys - 1) + 2 * bits + (levs - 1)
+    vmem = pl.BlockSpec(memory_space=pltpu.VMEM)
+    hbm = pl.BlockSpec(memory_space=pl.ANY)
     return pl.pallas_call(
-        weights_kernel,
-        name="weights",
+        functools.partial(analysis_weights_kernel, axes),
+        name="analysis_weights",
         out_shape=(
             jax.ShapeDtypeStruct((n, members), jnp.bfloat16),
             jax.ShapeDtypeStruct((n, LANES), jnp.float32),
             jax.ShapeDtypeStruct((n, members), jnp.bfloat16),
+            jax.ShapeDtypeStruct((levs, x_count, y_count // levs, lev_count, members), jnp.bfloat16),
         ),
-        in_specs=[pl.BlockSpec(memory_space=pltpu.VMEM)] * 3,
-        out_specs=tuple([pl.BlockSpec(memory_space=pltpu.VMEM)] * 3),
+        in_specs=[vmem, vmem, hbm, vmem, vmem],
+        out_specs=(vmem, vmem, vmem, hbm),
         scratch_shapes=[
+            pltpu.VMEM((n, members), jnp.float32),
+            pltpu.VMEM((edge, members), jnp.bfloat16),
+            pltpu.VMEM((edge, members), jnp.bfloat16),
+            pltpu.VMEM((gys - 1, part, members), jnp.float32),
+            pltpu.VMEM((gys * levs, part, members), jnp.bfloat16),
+            pltpu.VMEM((gys * levs, part, LANES), jnp.float32),
+            [pltpu.VMEM((n >> (b + 1), members), jnp.float32) for b in range(bits)],
             pltpu.VMEM((n, n), jnp.float32),
             pltpu.VMEM((n, members + LANES), jnp.float32),
             pltpu.VMEM((n, LANES), jnp.float32),
@@ -197,22 +308,25 @@
             pltpu.VMEM((BLOCK, LANES), jnp.float32),
             pltpu.VMEM((n // BLOCK, BLOCK, BLOCK), jnp.float32),
             pltpu.VMEM((n // BLOCK, n, BLOCK), jnp.float32),
+            pltpu.SemaphoreType.DMA((copies,)),
+            pltpu.SemaphoreType.DMA((copies,)),
+            pltpu.SemaphoreType.DMA((1,)),
         ],
-        compiler_params=pltpu.CompilerParams(vmem_limit_bytes=48 * 1024 * 1024),
-    )(hx, values[:, None], errors[:, None])
-
-
-def analyse(block, weight, hx_sum, values, errors):
+        compiler_params=pltpu.CompilerParams(
+            collective_id=0, has_side_effects=True, vmem_limit_bytes=48 * 1024 * 1024
+        ),
+    )(code, state.reshape(-1, members), state, values[:, None], errors[:, None])
+
+
+def analyse(block, weight, zmat, wvec, ybf):
     members = block.shape[-1]
-    zmat, wcol, ybf = weights(hx_sum, values, errors)
-    wvec = wcol[:, 0]
     xbar = jnp.mean(block, axis=-1, dtype=jnp.float32)
     anom = (block.astype(jnp.float32) - xbar[..., None]).astype(jnp.bfloat16)
     flat = anom.reshape(-1, members)
     cross = jnp.dot(flat, ybf.T, preferred_element_type=jnp.float32) / (
         members - 1
     )
-    n_obs = hx_sum.shape[0]
+    n_obs = ybf.shape[0]
     gain = (
         cross.reshape(block.shape[:-1] + (n_obs,)) * weight[:, :, None, :].astype(jnp.float32)
     ).astype(jnp.bfloat16)
@@ -225,13 +339,14 @@
 def local(state, obs_col, obs_row, foot_off, obs_lev, obs_val, obs_err, loc):
     level_groups = lax.axis_size("lev")
     ny_total = loc.shape[1] * lax.axis_size("gy") * level_groups
-    foot_code = footprint_code(obs_col, obs_row, foot_off, ny_total)
-    y_block = loc.shape[1]
-    relaid = relay(state)
-    y_start = (lax.axis_index("gy") * level_groups + lax.axis_index("lev")) * y_block
-    partial_sum = observe(relaid, y_start, foot_code, obs_lev, ny_total)
-    hx_sum = lax.psum(partial_sum, ("gy", "lev")) / KF
-    return analyse(relaid, loc, hx_sum, obs_val, obs_err)
+    x_count, y_count, lev_count, members = state.shape
+    code = footprint_code(
+        obs_col, obs_row, foot_off, obs_lev, (y_count, lev_count), ny_total,
+        lax.axis_index("gy") * y_count, lax.axis_index("lev") * lev_count,
+    )
+    zmat, wcol, ybf, relaid = analysis_weights(state, code, obs_val, obs_err)
+    block = relaid.transpose(1, 2, 0, 3, 4).reshape(x_count, loc.shape[1], -1, members)
+    return analyse(block, loc, zmat, wcol[:, 0], ybf)
 
 
 def solution(mesh):

time: 211 us -> 122 us (0.58)
  waiting for transfers between devices: 103 us -> 0 us
  Pallas kernels: 35.5 us -> 75.8 us
  between operations: 14.2 us -> 0.76 us
  starting transfers between devices: 6.7 us -> 0 us
  matrix products: 12.2 us -> 7.72 us
  other arithmetic: 11.4 us -> 7.49 us
  local copies, waits for them, and re-layouts: 27.2 us -> 29.5 us
    psum x1 -> x0, waiting for transfers between devices: 85.5 us -> none  [local(): hx_sum = lax.psum(partial_sum, ('gy', 'lev')) / KF]
    pallas_call x1, Pallas kernels: 35.5 us -> 75.8 us  [analysis_weights(): pl.pallas_call(functools.partial(analysis_weights_kernel, axes), name='an...]
    all_to_all x1 -> x0, waiting for transfers between devices: 16.5 us -> none  [relay(): return lax.all_to_all(state, 'lev', split_axis=1, concat_axis=2, tiled=True)]
    convert_element_type x1 -> x2, local copies, waits for them, and re-layouts: 6.15 us -> 10.6 us  [analyse(): xbar = jnp.mean(block, axis=-1, dtype=jnp.float32)]
    all_to_all x1 -> x0, starting transfers between devices: 4.37 us -> none  [relay(): return lax.all_to_all(state, 'lev', split_axis=1, concat_axis=2, tiled=True)]
    all_to_all x1 -> x0, local copies, waits for them, and re-layouts: 4.14 us -> none  [relay(): return lax.all_to_all(state, 'lev', split_axis=1, concat_axis=2, tiled=True)]
    reshape x0 -> x1, local copies, waits for them, and re-layouts: none -> 4.1 us  [analysis_weights(): state.reshape(-1, members)]
    unnamed x17 -> x9, local copies, waits for them, and re-layouts: 5.7 us -> 1.67 us
  transfers between devices with their start and end apart: 4 -> 0, of which waited for: 3 -> 0; matrix products, arithmetic and copies ran while one was open for 9% -> 0% of each run, Pallas kernels for 0% -> 0%
where the time goes in v1:
time: 122 us; the launch traced here: 121 us
  Pallas kernels  75.8 us (62%)
  local copies, waits for them, and re-layouts  29.5 us (24%)
  matrix products  7.72 us (6%)
  other arithmetic  7.49 us (6%)
    pallas_call x1, Pallas kernels, analysis_weights(): pl.pallas_call(functools.partial(analysis_weights_kernel, axes), name='an...  75.8 us
    convert_element_type x2, local copies, waits for them, and re-layouts, analyse(): xbar = jnp.mean(block, axis=-1, dtype=jnp.float32)  10.6 us
    mul x2, local copies, waits for them, and re-layouts, analyse(): cross.reshape(block.shape[:-1] + (n_obs,))  8.01 us
    dot_general x1, matrix products, analyse(): jnp.dot(flat, ybf.T, preferred_element_type=jnp.float32) / (members - 1)  5.11 us
    reshape x1, local copies, waits for them, and re-layouts, analysis_weights(): state.reshape(-1, members)  4.1 us
    div x3, local copies, waits for them, and re-layouts, analyse(): xbar = jnp.mean(block, axis=-1, dtype=jnp.float32)  2.82 us
    dot_general x1, matrix products, analyse(): jnp.dot(gain.reshape(-1, n_obs), zmat, preferred_element_type=jnp.float32)  2.62 us

profile of v1, /device:TPU:0, one launch (start us, length us, event | category | flops | bytes accessed | tf_op | source)
XLA Modules:
  0.0 121.3 jit_solution(16618808336422801849)
XLA Ops:
  0.6 0.7 broadcast_compare_fusion.1
  1.3 0.7 broadcast_divide_fusion
  2.1 0.1 copy.62
  2.2 0.1 copy.61
  2.3 0.8 copy.63.val_ref
  3.2 0.8 copy.64.err_ref
  4.0 0.8 copy.53
  4.8 1.5 %add_select_fusion.1.code_ref = s32[512,8]{1,0:T(8,128)S(1)} fusion(s32[512,8]{1,0:T(8,128)S(1)} %copy.61, s32[512,8]{1,0:T(8,128)S(1)} %copy.62, s32[512,8]{1,0:T(8,128)S(1)} %copy.53, s32[512]{0:T(512)S(1)} %get-tuple-element.13, s32[512]{0:T(512)} %param.9, s32[]{:T(128)S(6)} %mul.35, s32[512]{0:T(512)} %param.10, ...), kind=kLoop, calls=%fused_computation.13 | loop fusion | flops 110592 | bytes 72708 | tf_op jit(solution)/shard_map/jit(_where)/select_n | solution.py:28
  6.3 4.1 %reshape.44.state_ref = bf16[2048,512]{1,0:T(8,128)(2,1)} reshape(bf16[128,8,2,512]{3,2,1,0:T(2,128)(2,1)} %raw_ref.1) | data formatting | bytes 4194304 | tf_op jit(solution)/shard_map/reshape | solution.py:318
  10.4 75.8 %analysis_weights.1 = (bf16[512,512]{1,0:T(8,128)(2,1)S(1)}, f32[512,128]{1,0:T(8,128)S(1)}, bf16[512,512]{1,0:T(8,128)(2,1)S(1)}, bf16[4,128,2,2,512]{4,3,2,1,0:T(2,128)(2,1)S(1)}) custom-call(s32[512,8]{1,0:T(8,128)S(1)} %add_select_fusion.1.code_ref, bf16[2048,512]{1,0:T(8,128)(2,1)} %reshape.44.state_ref, bf16[128,8,2,512]{3,2,1,0:T(2,128)(2,1)} %raw_ref.1, ...), custom_call_target="tpu_custom_call" | custom-call | tf_op jit(solution)/shard_map/analysis_weights/pallas_call | solution.py:285
  86.3 0.0 copy-start
  86.3 0.8 copy-done
  87.1 0.1 slice_reduce_fusion
  87.2 2.2 %convert_reduce_fusion = f32[4,128,2,2]{3,2,1,0:T(2,128)S(1)} fusion(bf16[4,128,2,2,512]{4,3,2,1,0:T(2,128)(2,1)S(1)} %get-tuple-element.6), kind=kLoop, calls=%fused_computation.1 | loop fusion | flops 2095104 | bytes 2105344 | tf_op jit(solution)/shard_map/reduce_sum | solution.py:323
  89.5 0.3 multiply_bitcast_fusion
  89.7 0.2 copy.65
  89.9 1.1 copy.67
  91.1 1.5 %div.29 = f32[2048]{0:T(1024)S(1)} reshape(f32[128,2,4,2]{3,2,1,0:T(4,128)} %copy.67) | data formatting | bytes 16384 | tf_op jit(solution)/shard_map/div | solution.py:323
  92.6 1.5 %convert_bitcast_fusion = f32[128,2,4,2,512]{4,3,1,0,2:T(2,128)S(1)} fusion(bf16[4,128,2,2,512]{4,3,2,1,0:T(2,128)(2,1)S(1)} %get-tuple-element.6), kind=kLoop, calls=%fused_computation | loop fusion | flops 1048576 | bytes 6291456 | tf_op jit(solution)/shard_map/convert_element_type | solution.py:323
  94.0 4.5 %copy.66 = f32[128,2,4,2,512]{4,3,2,1,0:T(2,128)} copy(f32[128,2,4,2,512]{4,3,1,0,2:T(2,128)S(1)} %convert_bitcast_fusion) | data formatting | bytes 8388608 | tf_op jit(solution)/shard_map/convert_element_type | solution.py:323
  98.5 0.0 copy-start.3
  98.5 6.1 %reshape.46 = f32[2048,512]{1,0:T(8,128)} reshape(f32[128,2,4,2,512]{4,3,2,1,0:T(2,128)} %copy.66) | data formatting | bytes 8388608 | tf_op jit(solution)/shard_map/convert_element_type | solution.py:323
  104.6 0.0 copy-done.3
  104.6 2.6 %mul.39 = f32[128,2,8,512]{3,2,1,0:T(8,128)} broadcast(bf16[128,2,512]{2,1,0:T(2,128)(2,1)S(1)} %copy-done.3), dimensions={0,1,3} | broadcast | bytes 4456448 | tf_op jit(solution)/shard_map/mul | solution.py:331
  107.2 5.4 %copy.68 = f32[2048,512]{0,1:T(8,128)} copy(f32[2048,512]{1,0:T(8,128)} %bitcast.12) | data formatting | bytes 8388608 | tf_op jit(solution)/shard_map/mul | solution.py:331
  112.7 0.0 copy-start.1
  112.7 0.0 copy-start.2
  112.7 5.1 %multiply_reduce_fusion = (f32[2048]{0:T(1024)S(1)}, bf16[2048,512]{0,1:T(8,128)(2,1)S(1)}) fusion(f32[512]{0:T(512)S(1)} %slice_reduce_fusion, f32[2048,512]{0,1:T(8,128)} %copy.68, bf16[512,512]{1,0:T(8,128)(2,1)S(1)} %get-tuple-element.7, f32[2048,512]{1,0:T(8,128)} %reshape.46, f32[2048]{0:T(1024)S(1)} %div.29), kind=kOutput, calls=%fused_computation.3 | convolution fusion | flops 1082128384 | bytes 11028480 | tf_op jit(solution)/shard_map/dot_general | solution.py:326
  117.8 0.0 copy-done.1
  117.8 0.0 copy-done.2
  117.8 2.6 %subtract_convert_fusion = bf16[2048,512]{1,0:T(8,128)(2,1)} fusion(bf16[2048,512]{0,1:T(8,128)(2,1)S(1)} %get-tuple-element.17, bf16[512,512]{1,0:T(8,128)(2,1)S(1)} %copy-done.1, f32[2048,512]{1,0:T(8,128)S(1)} %copy-done.2, f32[2048]{0:T(1024)S(1)} %div.29), kind=kOutput, calls=%fused_computation.2 | convolution fusion | flops 1078984704 | bytes 8921088 | tf_op jit(solution)/shard_map/dot_general | solution.py:334
  120.4 0.2 reduce_sum.22
  120.6 0.1 copy.69
  120.7 0.6 add.51
  (1 shorter events, 0.0 us)
Async XLA Ops:
  86.3 0.8 copy-start
  98.5 6.1 %copy-start.3 = (bf16[128,2,512]{2,1,0:T(2,128)(2,1)S(1)}, bf16[128,2,512]{2,1,0:T(2,128)(2,1)}, u32[]{:S(2)}) copy-start(bf16[128,2,512]{2,1,0:T(2,128)(2,1)} %param.15) | copy-start | bytes 786436
  112.7 5.1 %copy-start.1 = (bf16[512,512]{1,0:T(8,128)(2,1)S(1)}, bf16[512,512]{1,0:T(8,128)(2,1)}, u32[]{:S(2)}) copy-start(bf16[512,512]{1,0:T(8,128)(2,1)} %copy-done) | copy-start | bytes 1572868
  112.7 5.1 %copy-start.2 = (f32[2048,512]{1,0:T(8,128)S(1)}, f32[2048,512]{1,0:T(8,128)}, u32[]{:S(2)}) copy-start(f32[2048,512]{1,0:T(8,128)} %reshape.46) | copy-start | bytes 12582916

commit v2 on v1

--- a/solution.py
+++ b/solution.py
@@ -17,15 +17,21 @@
 
 
 def footprint_code(obs_col, obs_row, foot_off, obs_lev, shape, ny_total, y_start, lev_start):
-    y_count, lev_count = shape
+    x_count, y_count, lev_count = shape
+    planes = y_count * lev_count
     span = 2 * DY + 1
     shift_x = foot_off // span - HW
     shift_y = foot_off % span - DY
-    x_ext = obs_col[:, None] + shift_x + HW
+    x_here = obs_col[:, None] + shift_x
     y_here = jnp.clip(obs_row[:, None] + shift_y, 0, ny_total - 1) - y_start
     lev_here = obs_lev[:, None] - lev_start
     inside = (y_here >= 0) & (y_here < y_count) & (lev_here >= 0) & (lev_here < lev_count)
-    return jnp.where(inside, (x_ext * y_count + y_here) * lev_count + lev_here, -1)
+    plane = y_here * lev_count + lev_here
+    middle = plane * x_count + x_here
+    before = planes * x_count + plane * HW + x_here + HW
+    after = planes * (x_count + HW) + plane * HW + x_here - x_count
+    spot = jnp.where(x_here < 0, before, jnp.where(x_here < x_count, middle, after))
+    return jnp.where(inside, spot, -1)
 
 
 def lane_cast(value, k):
@@ -144,15 +150,16 @@
 
 
 def analysis_weights_kernel(
-    axes, code_ref, state_ref, raw_ref, val_ref, err_ref, z_ref, w_out_ref, y_ref, relaid_ref,
+    axes, code_ref, state_ref, val_ref, err_ref, z_ref, w_out_ref, y_ref, relaid_ref,
     acc_ref, before_ref, after_ref, zin_ref, ys_ref, hb_ref, half_refs,
     a_ref, s_ref, root_ref, w_ref, x_ref, inv_ref, low_ref, send_sem, recv_sem, own_sem,
 ):
     gxs, gys, levs = axes
     gx, gy, lev = lax.axis_index("gx"), lax.axis_index("gy"), lax.axis_index("lev")
     n, members = acc_ref.shape
-    edge = before_ref.shape[0]
-    inner = state_ref.shape[0]
+    planes, x_count = state_ref.shape[:2]
+    edge, inner = planes * HW, planes * x_count
+    share = planes // levs
     right, left = lax.rem(gx + 1, gxs), lax.rem(gx + gxs - 1, gxs)
     levels = [(lax.rem(lev + d, levs)) for d in range(1, levs)]
     lats = [(lax.rem(gy + d, gys)) for d in range(1, gys)]
@@ -172,13 +179,12 @@
         )
 
     halo = [
-        remote(state_ref.at[inner - edge : inner], before_ref, {"gx": right}),
-        remote(state_ref.at[0:edge], after_ref, {"gx": left}),
+        remote(state_ref.at[:, x_count - HW :], before_ref, {"gx": right}),
+        remote(state_ref.at[:, :HW], after_ref, {"gx": left}),
     ]
     for copy in halo:
         copy.start()
-    y_block = relaid_ref.shape[2]
-    own = pltpu.make_async_copy(raw_ref.at[:, pl.ds(lev * y_block, y_block)], relaid_ref.at[lev], own_sem.at[0])
+    own = pltpu.make_async_copy(state_ref.at[pl.ds(lev * share, share)], relaid_ref.at[lev], own_sem.at[0])
     own.start()
 
     def chosen(base, width):
@@ -188,22 +194,23 @@
             hits = hits + jnp.where(code_ref[:, slot : slot + 1] == spot, 1.0, 0.0)
         return hits.astype(jnp.bfloat16)
 
+    def flat(ref):
+        return ref[...].astype(jnp.float32).reshape(edge, members).astype(jnp.bfloat16)
+
     acc_ref[...] = jnp.zeros_like(acc_ref)
-    width = 256
 
     def pick(i, carry):
-        at = pl.multiple_of(i * width, width)
         acc_ref[...] += jnp.dot(
-            chosen(edge + at, width), state_ref[pl.ds(at, width), :], preferred_element_type=jnp.float32
+            chosen(i * x_count, x_count), state_ref[i], preferred_element_type=jnp.float32
         )
         return carry
 
-    lax.fori_loop(0, inner // width, pick, 0)
-    sel_before, sel_after = chosen(0, edge), chosen(edge + inner, edge)
+    lax.fori_loop(0, planes, pick, 0)
+    sel_before, sel_after = chosen(inner, edge), chosen(inner + edge, edge)
     for copy in halo:
         copy.wait()
-    acc_ref[...] += jnp.dot(sel_before, before_ref[...], preferred_element_type=jnp.float32) + jnp.dot(
-        sel_after, after_ref[...], preferred_element_type=jnp.float32
+    acc_ref[...] += jnp.dot(sel_before, flat(before_ref), preferred_element_type=jnp.float32) + jnp.dot(
+        sel_after, flat(after_ref), preferred_element_type=jnp.float32
     )
     base, size = 0, n
     bits = levs.bit_length() - 1
@@ -258,7 +265,7 @@
         for copy in copies:
             copy.wait()
     copies = [
-        remote(raw_ref.at[:, pl.ds(v * y_block, y_block)], relaid_ref.at[lev], {"lev": v}) for v in levels
+        remote(state_ref.at[pl.ds(v * share, share)], relaid_ref.at[lev], {"lev": v}) for v in levels
     ]
     for copy in copies:
         copy.start()
@@ -274,9 +281,8 @@
 def analysis_weights(state, code, values, errors):
     axes = tuple(lax.axis_size(name) for name in ("gx", "gy", "lev"))
     gxs, gys, levs = axes
-    x_count, y_count, lev_count, members = state.shape
+    planes, x_count, members = state.shape
     n = values.shape[0]
-    edge = HW * y_count * lev_count
     part = n // (gys * levs)
     bits = levs.bit_length() - 1
     copies = 2 + bits + (gys - 1) + 2 * (gys - 1) + 2 * bits + (levs - 1)
@@ -289,14 +295,14 @@
             jax.ShapeDtypeStruct((n, members), jnp.bfloat16),
             jax.ShapeDtypeStruct((n, LANES), jnp.float32),
             jax.ShapeDtypeStruct((n, members), jnp.bfloat16),
-            jax.ShapeDtypeStruct((levs, x_count, y_count // levs, lev_count, members), jnp.bfloat16),
+            jax.ShapeDtypeStruct((levs, planes // levs, x_count, members), jnp.bfloat16),
         ),
-        in_specs=[vmem, vmem, hbm, vmem, vmem],
+        in_specs=[vmem, vmem, vmem, vmem],
         out_specs=(vmem, vmem, vmem, hbm),
         scratch_shapes=[
             pltpu.VMEM((n, members), jnp.float32),
-            pltpu.VMEM((edge, members), jnp.bfloat16),
-            pltpu.VMEM((edge, members), jnp.bfloat16),
+            pltpu.VMEM((planes, HW, members), jnp.bfloat16),
+            pltpu.VMEM((planes, HW, members), jnp.bfloat16),
             pltpu.VMEM((gys - 1, part, members), jnp.float32),
             pltpu.VMEM((gys * levs, part, members), jnp.bfloat16),
             pltpu.VMEM((gys * levs, part, LANES), jnp.float32),
@@ -315,25 +321,80 @@
         compiler_params=pltpu.CompilerParams(
             collective_id=0, has_side_effects=True, vmem_limit_bytes=48 * 1024 * 1024
         ),
-    )(code, state.reshape(-1, members), state, values[:, None], errors[:, None])
-
-
-def analyse(block, weight, zmat, wvec, ybf):
-    members = block.shape[-1]
-    xbar = jnp.mean(block, axis=-1, dtype=jnp.float32)
-    anom = (block.astype(jnp.float32) - xbar[..., None]).astype(jnp.bfloat16)
-    flat = anom.reshape(-1, members)
-    cross = jnp.dot(flat, ybf.T, preferred_element_type=jnp.float32) / (
-        members - 1
+    )(code, state, values[:, None], errors[:, None])
+
+
+def analyse_kernel(relaid_ref, loc_ref, z_ref, y_ref, w_ref, mean_ref, out_ref, rows_ref):
+    levs, share, width, members = relaid_ref.shape
+    lats = loc_ref.shape[0]
+    pairs = share // lats
+    stride = lats * levs * pairs
+    block = relaid_ref[...].reshape(levs * share * width, members).astype(jnp.float32)
+    xbar = jnp.mean(block, axis=1, keepdims=True)
+    anom = (block - xbar).astype(jnp.bfloat16)
+    cross = lax.dot_general(
+        anom, y_ref[...], (((1,), (1,)), ((), ())), preferred_element_type=jnp.float32
+    ) * (1.0 / (members - 1))
+    parts = []
+    for lev in range(levs):
+        for lat in range(lats):
+            weight = loc_ref[lat].astype(jnp.float32)
+            for pair in range(pairs):
+                at = (lev * share + lat * pairs + pair) * width
+                parts.append((cross[at : at + width] * weight).astype(jnp.bfloat16))
+    gain = jnp.concatenate(parts, axis=0)
+    mean = xbar + jnp.sum(gain.astype(jnp.float32) * w_ref[...], axis=1, keepdims=True)
+    update = jnp.dot(gain, z_ref[...], preferred_element_type=jnp.float32)
+    result = anom.astype(jnp.float32) - update
+    lane = lax.broadcasted_iota(jnp.int32, (width, LANES), 1)
+    means = jnp.zeros((width, LANES), jnp.float32)
+    for lev in range(levs):
+        for lat in range(lats):
+            for pair in range(pairs):
+                at = (lev * share + lat * pairs + pair) * width
+                spot = lat * levs * pairs + lev * pairs + pair
+                means = jnp.where(lane == spot, jnp.broadcast_to(mean[at : at + width], (width, LANES)), means)
+                for c in range(members // LANES):
+                    rows_ref[c, pl.ds(spot, width, stride=stride), :] = result[
+                        at : at + width, c * LANES : (c + 1) * LANES
+                    ]
+    mean_ref[...] = means
+    for c in range(members // LANES):
+        out_ref[:, c * LANES : (c + 1) * LANES] = rows_ref[c].astype(jnp.bfloat16)
+
+
+def analyse(relaid, loc, zmat, wvec, ybf):
+    levs, share, x_count, members = relaid.shape
+    lats, n = loc.shape[1], ybf.shape[0]
+    planes = levs * share
+    width = min(32, x_count)
+    means, out = pl.pallas_call(
+        analyse_kernel,
+        name="analyse",
+        grid=(x_count // width,),
+        out_shape=(
+            jax.ShapeDtypeStruct((x_count, LANES), jnp.float32),
+            jax.ShapeDtypeStruct((x_count * planes, members), jnp.bfloat16),
+        ),
+        in_specs=[
+            pl.BlockSpec((levs, share, width, members), lambda i: (0, 0, i, 0)),
+            pl.BlockSpec((lats, width, n), lambda i: (0, i, 0)),
+            pl.BlockSpec((n, members), lambda i: (0, 0)),
+            pl.BlockSpec((n, members), lambda i: (0, 0)),
+            pl.BlockSpec((1, n), lambda i: (0, 0)),
+        ],
+        out_specs=(
+            pl.BlockSpec((width, LANES), lambda i: (i, 0)),
+            pl.BlockSpec((width * planes, members), lambda i: (i, 0)),
+        ),
+        scratch_shapes=[pltpu.VMEM((members // LANES, width * planes, LANES), jnp.float32)],
+        compiler_params=pltpu.CompilerParams(vmem_limit_bytes=48 * 1024 * 1024),
+    )(relaid, loc.transpose(1, 0, 2), zmat, ybf, wvec[None, :])
+    per_lat = planes // lats
+    return (
+        means[:, :planes].reshape(x_count, lats, per_lat),
+        out.reshape(x_count, lats, per_lat, members),
     )
-    n_obs = ybf.shape[0]
-    gain = (
-        cross.reshape(block.shape[:-1] + (n_obs,)) * weight[:, :, None, :].astype(jnp.float32)
-    ).astype(jnp.bfloat16)
-    mean_part = xbar + jnp.sum(gain.astype(jnp.float32) * wvec, axis=-1)
-    update = jnp.dot(gain.reshape(-1, n_obs), zmat, preferred_element_type=jnp.float32)
-    anom_part = (flat.astype(jnp.float32) - update).astype(jnp.bfloat16).reshape(block.shape)
-    return (mean_part, anom_part)
 
 
 def local(state, obs_col, obs_row, foot_off, obs_lev, obs_val, obs_err, loc):
@@ -341,12 +402,12 @@
     ny_total = loc.shape[1] * lax.axis_size("gy") * level_groups
     x_count, y_count, lev_count, members = state.shape
     code = footprint_code(
-        obs_col, obs_row, foot_off, obs_lev, (y_count, lev_count), ny_total,
+        obs_col, obs_row, foot_off, obs_lev, (x_count, y_count, lev_count), ny_total,
         lax.axis_index("gy") * y_count, lax.axis_index("lev") * lev_count,
     )
-    zmat, wcol, ybf, relaid = analysis_weights(state, code, obs_val, obs_err)
-    block = relaid.transpose(1, 2, 0, 3, 4).reshape(x_count, loc.shape[1], -1, members)
-    return analyse(block, loc, zmat, wcol[:, 0], ybf)
+    planes = state.transpose(1, 2, 0, 3).reshape(y_count * lev_count, x_count, members)
+    zmat, wcol, ybf, relaid = analysis_weights(planes, code, obs_val, obs_err)
+    return analyse(relaid, loc, zmat, wcol[:, 0], ybf)
 
 
 def solution(mesh):

time: 122 us -> 99.2 us (0.81)
  local copies, waits for them, and re-layouts: 29.5 us -> 6.31 us
  Pallas kernels: 75.8 us -> 88.5 us
  matrix products: 7.72 us -> 0 us
  other arithmetic: 7.49 us -> 2.98 us
    convert_element_type x2 -> x0, local copies, waits for them, and re-layouts: 10.6 us -> none  [analyse(): xbar = jnp.mean(block, axis=-1, dtype=jnp.float32)]
    mul x2 -> x0, local copies, waits for them, and re-layouts: 8.01 us -> none  [analyse(): cross.reshape(block.shape[:-1] + (n_obs,))]
    dot_general x2 -> x0, matrix products: 7.72 us -> none  [the longest x1 5.11 us: analyse(): jnp.dot(flat, ybf.T, preferred_element_type=jnp.float32) / (members - 1)]
    pallas_call x1, Pallas kernels: 75.8 us -> 82.3 us  [analysis_weights(): pl.pallas_call(functools.partial(analysis_weights_kernel, axes), name='an...]
    pallas_call x0 -> x1, Pallas kernels: none -> 6.18 us  [analyse(): pl.pallas_call(analyse_kernel, name='analyse', grid=(x_count // width,),...]
    reshape x1 -> x0, local copies, waits for them, and re-layouts: 4.1 us -> none  [analysis_weights(): state.reshape(-1, members)]
    transpose x0 -> x1, local copies, waits for them, and re-layouts: none -> 4.08 us  [local(): state.transpose(1, 2, 0, 3).reshape(y_count * lev_count, x_count, members)]
    div x3 -> x0, local copies, waits for them, and re-layouts: 2.82 us -> none  [analyse(): xbar = jnp.mean(block, axis=-1, dtype=jnp.float32)]
where the time goes in v2:
time: 99.2 us; the launch traced here: 98.5 us
  Pallas kernels  88.5 us (89%)
  local copies, waits for them, and re-layouts  6.31 us (6%)
  other arithmetic  2.98 us (3%)
    pallas_call x1, Pallas kernels, analysis_weights(): pl.pallas_call(functools.partial(analysis_weights_kernel, axes), name='an...  82.3 us
    pallas_call x1, Pallas kernels, analyse(): pl.pallas_call(analyse_kernel, name='analyse', grid=(x_count // width,),...  6.18 us
    transpose x1, local copies, waits for them, and re-layouts, local(): state.transpose(1, 2, 0, 3).reshape(y_count * lev_count, x_count, members)  4.08 us

profile of v2, /device:TPU:0, one launch (start us, length us, event | category | flops | bytes accessed | tf_op | source)
XLA Modules:
  0.0 98.5 jit_solution(3858369825421166011)
XLA Ops:
  0.6 0.7 broadcast_compare_fusion.1
  1.3 0.7 broadcast_divide_fusion
  2.1 0.1 copy.38
  2.2 0.1 copy.39
  2.3 0.8 copy.30
  3.2 1.6 %select_select_fusion.code_ref = s32[512,8]{1,0:T(8,128)S(1)} fusion(s32[512,8]{1,0:T(8,128)S(1)} %copy.38, s32[512,8]{1,0:T(8,128)S(1)} %copy.39, s32[512,8]{1,0:T(8,128)S(1)} %copy.30, s32[512]{0:T(512)S(1)} %get-tuple-element.17, s32[512]{0:T(512)} %param.9, s32[]{:T(128)S(6)} %mul.16, s32[512]{0:T(512)} %param.10, ...), kind=kLoop, calls=%fused_computation.7 | loop fusion | flops 151552 | bytes 72708 | tf_op jit(solution)/shard_map/jit(_where)/select_n | solution.py:34
  4.7 0.0 copy-start.1
  4.8 0.0 copy-start.2
  4.8 4.1 %copy.41 = bf16[8,2,128,512]{3,2,1,0:T(8,128)(2,1)} copy(bf16[8,2,128,512]{3,1,0,2:T(2,128)(2,1)} %bitcast.15) | data formatting | bytes 4194304 | tf_op jit(solution)/shard_map/transpose | solution.py:408
  8.8 0.0 copy-start
  8.8 0.0 copy-done.1
  8.8 0.1 copy.42.val_ref
  9.0 0.0 copy-done.2
  9.0 0.1 copy.43.err_ref
  9.2 82.3 %analysis_weights.1 = (bf16[512,512]{1,0:T(8,128)(2,1)S(1)}, f32[512,128]{1,0:T(8,128)S(1)}, bf16[512,512]{1,0:T(8,128)(2,1)S(1)}, bf16[4,4,128,512]{3,2,1,0:T(8,128)(2,1)S(1)}) custom-call(s32[512,8]{1,0:T(8,128)S(1)} %select_select_fusion.code_ref, bf16[16,128,512]{2,1,0:T(8,128)(2,1)} %bitcast.14, f32[512,1]{1,0:T(8,128)S(1)} %copy.42.val_ref, ...), custom_call_target="tpu_custom_call" | custom-call | tf_op jit(solution)/shard_map/analysis_weights/pallas_call | solution.py:291
  91.5 0.1 slice_reduce_fusion
  91.6 0.0 copy-done
  91.7 6.2 %analyse.1 = (f32[128,128]{1,0:T(8,128)S(1)}, bf16[2048,512]{1,0:T(8,128)(2,1)}) custom-call(bf16[4,4,128,512]{3,2,1,0:T(8,128)(2,1)S(1)} %get-tuple-element.8.relaid_ref, bf16[2,128,512]{2,1,0:T(8,128)(2,1)S(1)} %bitcast.11, bf16[512,512]{1,0:T(8,128)(2,1)S(1)} %get-tuple-element.9.z_ref, bf16[512,512]{1,0:T(8,128)(2,1)S(1)} %get-tuple-element.10.y_ref, ...), custom_call_target="tpu_custom_call" | custom-call | tf_op jit(solution)/shard_map/analyse/pallas_call | solution.py:371
  97.9 0.7 copy.45
  (2 shorter events, 0.0 us)
Async XLA Ops:
  4.7 4.1 %copy-start.1 = (f32[512]{0:T(512)S(1)}, f32[512]{0:T(512)}, u32[]{:S(2)}) copy-start(f32[512]{0:T(512)} %param.13) | copy-start | bytes 6148
  4.8 4.2 %copy-start.2 = (f32[512]{0:T(512)S(1)}, f32[512]{0:T(512)}, u32[]{:S(2)}) copy-start(f32[512]{0:T(512)} %param.14) | copy-start | bytes 6148
  8.8 82.8 %copy-start = (bf16[128,2,512]{2,1,0:T(2,128)(2,1)S(1)}, bf16[128,2,512]{2,1,0:T(2,128)(2,1)}, u32[]{:S(2)}) copy-start(bf16[128,2,512]{2,1,0:T(2,128)(2,1)} %param.15) | copy-start | bytes 786436

commit v3 on v2

--- a/solution.py
+++ b/solution.py
@@ -46,6 +46,17 @@
     return lax.dot_general(
         a, b, (dims, ((), ())), precision=lax.Precision.HIGHEST, preferred_element_type=jnp.float32
     )
+
+
+def split_dot(a, b, dims):
+    a_high, b_high = a.astype(jnp.bfloat16), b.astype(jnp.bfloat16)
+    a_low = (a - a_high.astype(jnp.float32)).astype(jnp.bfloat16)
+    b_low = (b - b_high.astype(jnp.float32)).astype(jnp.bfloat16)
+
+    def dot(left, right):
+        return lax.dot_general(left, right, (dims, ((), ())), preferred_element_type=jnp.float32)
+
+    return dot(a_high, b_high) + (dot(a_high, b_low) + dot(a_low, b_high))
 
 
 def factor_block(w_ref, x_ref, root_err):
@@ -134,7 +145,7 @@
                     low_ref[kk, end:, :] = below
                     a_ref[end:, left:] = a_ref[end:, left:] - f32_dot(below, panel, ((1,), (1,)))
                     load_block(end)
-                    s_ref[end:, :] = s_ref[end:, :] - f32_dot(below, s_ref[at:end, :], ((1,), (0,)))
+                    s_ref[end:, :] = s_ref[end:, :] - split_dot(below, s_ref[at:end, :], ((1,), (0,)))
 
         return carry
 
@@ -143,7 +154,7 @@
         at, end = kk * BLOCK, (kk + 1) * BLOCK
         right = s_ref[at:end, :]
         if end < n:
-            right = right - f32_dot(low_ref[kk, end:, :], s_ref[end:, :], ((0,), (0,)))
+            right = right - split_dot(low_ref[kk, end:, :], s_ref[end:, :], ((0,), (0,)))
         s_ref[at:end, :] = f32_dot(inv_ref[kk], right, ((0,), (0,)))
     z_ref[...] = s_ref[:, :members].astype(jnp.bfloat16)
     w_out_ref[...] = s_ref[:, members:]
@@ -199,13 +210,16 @@
 
     acc_ref[...] = jnp.zeros_like(acc_ref)
 
+    batch = 4 if planes % 4 == 0 else 1
+
     def pick(i, carry):
+        rows = state_ref[pl.ds(i * batch, batch)].reshape(batch * x_count, members)
         acc_ref[...] += jnp.dot(
-            chosen(i * x_count, x_count), state_ref[i], preferred_element_type=jnp.float32
+            chosen(i * (batch * x_count), batch * x_count), rows, preferred_element_type=jnp.float32
         )
         return carry
 
-    lax.fori_loop(0, planes, pick, 0)
+    lax.fori_loop(0, planes // batch, pick, 0)
     sel_before, sel_after = chosen(inner, edge), chosen(inner + edge, edge)
     for copy in halo:
         copy.wait()
@@ -245,7 +259,11 @@
     hbar = jnp.mean(hx, axis=1, keepdims=True)
     chunk = base // part + gy
     ys_ref[chunk] = (hx - hbar).astype(jnp.bfloat16)
-    hb_ref[chunk] = jnp.broadcast_to(hbar, (part, LANES))
+    diagonal = lax.broadcasted_iota(jnp.int32, (part, LANES), 0) == lax.broadcasted_iota(
+        jnp.int32, (part, LANES), 1
+    )
+    row = jnp.sum(jnp.where(diagonal, hbar, 0.0), axis=0, keepdims=True)
+    hb_ref[chunk] = jnp.broadcast_to(row, (SUB, LANES))
     copies = []
     for lat in lats:
         copies.append(remote(ys_ref.at[chunk], ys_ref.at[chunk], {"gy": lat}))
@@ -271,7 +289,12 @@
         copy.start()
     for c in range(levs * gys):
         s_ref[c * part : (c + 1) * part, :members] = ys_ref[c].astype(jnp.float32)
-        s_ref[c * part : (c + 1) * part, members:] = val_ref[c * part : (c + 1) * part, :] - hb_ref[c]
+        center = jnp.sum(
+            jnp.where(diagonal, jnp.broadcast_to(hb_ref[c][:1, :], (part, LANES)), 0.0), axis=1, keepdims=True
+        )
+        s_ref[c * part : (c + 1) * part, members:] = jnp.broadcast_to(
+            val_ref[c * part : (c + 1) * part, :] - center, (part, LANES)
+        )
     solve_weights(err_ref, z_ref, w_out_ref, y_ref, a_ref, s_ref, root_ref, w_ref, x_ref, inv_ref, low_ref)
     for copy in copies:
         copy.wait()
@@ -305,7 +328,7 @@
             pltpu.VMEM((planes, HW, members), jnp.bfloat16),
             pltpu.VMEM((gys - 1, part, members), jnp.float32),
             pltpu.VMEM((gys * levs, part, members), jnp.bfloat16),
-            pltpu.VMEM((gys * levs, part, LANES), jnp.float32),
+            pltpu.VMEM((gys * levs, SUB, LANES), jnp.float32),
             [pltpu.VMEM((n >> (b + 1), members), jnp.float32) for b in range(bits)],
             pltpu.VMEM((n, n), jnp.float32),
             pltpu.VMEM((n, members + LANES), jnp.float32),

time: 99.2 us -> 89.6 us (0.903)
  Pallas kernels: 88.5 us -> 79.2 us
    pallas_call x1, Pallas kernels: 82.3 us -> 73 us  [analysis_weights(): pl.pallas_call(functools.partial(analysis_weights_kernel, axes), name='an...]
where the time goes in v3:
time: 89.6 us; the launch traced here: 89.3 us
  Pallas kernels  79.2 us (88%)
  local copies, waits for them, and re-layouts  6.31 us (7%)
  other arithmetic  2.98 us (3%)
    pallas_call x1, Pallas kernels, analysis_weights(): pl.pallas_call(functools.partial(analysis_weights_kernel, axes), name='an...  73 us
    pallas_call x1, Pallas kernels, analyse(): pl.pallas_call(analyse_kernel, name='analyse', grid=(x_count // width,),...  6.19 us
    transpose x1, local copies, waits for them, and re-layouts, local(): state.transpose(1, 2, 0, 3).reshape(y_count * lev_count, x_count, members)  4.08 us

profile of v3, /device:TPU:0, one launch (start us, length us, event | category | flops | bytes accessed | tf_op | source)
XLA Modules:
  0.0 89.3 jit_solution(10895782915126623661)
XLA Ops:
  0.6 0.7 broadcast_compare_fusion.1
  1.3 0.7 broadcast_divide_fusion
  2.1 0.1 copy.38
  2.2 0.1 copy.39
  2.3 0.8 copy.30
  3.2 1.6 %select_select_fusion.code_ref = s32[512,8]{1,0:T(8,128)S(1)} fusion(s32[512,8]{1,0:T(8,128)S(1)} %copy.38, s32[512,8]{1,0:T(8,128)S(1)} %copy.39, s32[512,8]{1,0:T(8,128)S(1)} %copy.30, s32[512]{0:T(512)S(1)} %get-tuple-element.17, s32[512]{0:T(512)} %param.9, s32[]{:T(128)S(6)} %mul.16, s32[512]{0:T(512)} %param.10, ...), kind=kLoop, calls=%fused_computation.7 | loop fusion | flops 151552 | bytes 72708 | tf_op jit(solution)/shard_map/jit(_where)/select_n | solution.py:34
  4.7 0.0 copy-start.1
  4.8 0.0 copy-start.2
  4.8 4.1 %copy.41 = bf16[8,2,128,512]{3,2,1,0:T(8,128)(2,1)} copy(bf16[8,2,128,512]{3,1,0,2:T(2,128)(2,1)} %bitcast.15) | data formatting | bytes 4194304 | tf_op jit(solution)/shard_map/transpose | solution.py:431
  8.8 0.0 copy-start
  8.8 0.0 copy-done.1
  8.8 0.1 copy.42.val_ref
  9.0 0.0 copy-done.2
  9.0 0.1 copy.43.err_ref
  9.2 73.0 %analysis_weights.1 = (bf16[512,512]{1,0:T(8,128)(2,1)S(1)}, f32[512,128]{1,0:T(8,128)S(1)}, bf16[512,512]{1,0:T(8,128)(2,1)S(1)}, bf16[4,4,128,512]{3,2,1,0:T(8,128)(2,1)S(1)}) custom-call(s32[512,8]{1,0:T(8,128)S(1)} %select_select_fusion.code_ref, bf16[16,128,512]{2,1,0:T(8,128)(2,1)} %bitcast.14, f32[512,1]{1,0:T(8,128)S(1)} %copy.42.val_ref, ...), custom_call_target="tpu_custom_call" | custom-call | tf_op jit(solution)/shard_map/analysis_weights/pallas_call | solution.py:314
  82.2 0.1 slice_reduce_fusion
  82.3 0.0 copy-done
  82.4 6.2 %analyse.1 = (f32[128,128]{1,0:T(8,128)S(1)}, bf16[2048,512]{1,0:T(8,128)(2,1)}) custom-call(bf16[4,4,128,512]{3,2,1,0:T(8,128)(2,1)S(1)} %get-tuple-element.8.relaid_ref, bf16[2,128,512]{2,1,0:T(8,128)(2,1)S(1)} %bitcast.11, bf16[512,512]{1,0:T(8,128)(2,1)S(1)} %get-tuple-element.9.z_ref, bf16[512,512]{1,0:T(8,128)(2,1)S(1)} %get-tuple-element.10.y_ref, ...), custom_call_target="tpu_custom_call" | custom-call | tf_op jit(solution)/shard_map/analyse/pallas_call | solution.py:394
  88.6 0.7 copy.45
  (2 shorter events, 0.0 us)
Async XLA Ops:
  4.7 4.1 %copy-start.1 = (f32[512]{0:T(512)S(1)}, f32[512]{0:T(512)}, u32[]{:S(2)}) copy-start(f32[512]{0:T(512)} %param.13) | copy-start | bytes 6148
  4.8 4.2 %copy-start.2 = (f32[512]{0:T(512)S(1)}, f32[512]{0:T(512)}, u32[]{:S(2)}) copy-start(f32[512]{0:T(512)} %param.14) | copy-start | bytes 6148
  8.8 73.5 %copy-start = (bf16[128,2,512]{2,1,0:T(2,128)(2,1)S(1)}, bf16[128,2,512]{2,1,0:T(2,128)(2,1)}, u32[]{:S(2)}) copy-start(bf16[128,2,512]{2,1,0:T(2,128)(2,1)} %param.15) | copy-start | bytes 786436

commit v4 on v3

--- a/solution.py
+++ b/solution.py
@@ -13,6 +13,7 @@
 SUB = 8
 LANES = 128
 BLOCK = 64
+PIPE = 2
 MESH = pl.DeviceIdType.MESH
 
 
@@ -228,29 +229,46 @@
     )
     base, size = 0, n
     bits = levs.bit_length() - 1
-    bases = []
+    lanes = [slice(c * members // PIPE, (c + 1) * members // PIPE) for c in range(PIPE)]
+    bases, flying = [], [[] for _ in lanes]
     for b in range(bits):
         size //= 2
         bit = lax.rem(lev // (1 << b), 2)
         partner = lev + (1 - 2 * bit) * (1 << b)
         keep, give = base + bit * size, base + (1 - bit) * size
-        copy = remote(acc_ref.at[pl.ds(pl.multiple_of(give, 8), size)], half_refs[b], {"lev": partner})
-        copy.start()
-        copy.wait()
-        rows = pl.ds(pl.multiple_of(keep, 8), size)
-        acc_ref[rows, :] = acc_ref[rows, :] + half_refs[b][...]
+        for c, cols in enumerate(lanes):
+            for copy in flying[c]:
+                copy.wait()
+            if b:
+                rows = pl.ds(pl.multiple_of(base, 8), size * 2)
+                acc_ref[rows, cols] = acc_ref[rows, cols] + half_refs[b - 1][:, cols]
+            copy = remote(
+                acc_ref.at[pl.ds(pl.multiple_of(give, 8), size), cols], half_refs[b].at[:, cols], {"lev": partner}
+            )
+            copy.start()
+            flying[c] = [copy]
         base = keep
         bases.append((base, size, partner))
     part = n // (levs * gys)
-    copies = []
-    for d, lat in enumerate(lats):
-        copies.append(
-            remote(acc_ref.at[pl.ds(pl.multiple_of(base + lat * part, 8), part)], zin_ref.at[d], {"gy": lat})
-        )
-    for copy in copies:
-        copy.start()
-    for copy in copies:
-        copy.wait()
+    for c, cols in enumerate(lanes):
+        for copy in flying[c]:
+            copy.wait()
+        if bits:
+            rows = pl.ds(pl.multiple_of(base, 8), size)
+            acc_ref[rows, cols] = acc_ref[rows, cols] + half_refs[bits - 1][:, cols]
+        flying[c] = [
+            remote(
+                acc_ref.at[pl.ds(pl.multiple_of(base + lat * part, 8), part), cols],
+                zin_ref.at[d, :, cols],
+                {"gy": lat},
+            )
+            for d, lat in enumerate(lats)
+        ]
+        for copy in flying[c]:
+            copy.start()
+    for copies in flying:
+        for copy in copies:
+            copy.wait()
     mine = base + gy * part
     total = acc_ref[pl.ds(pl.multiple_of(mine, 8), part), :]
     for d in range(gys - 1):
@@ -308,7 +326,7 @@
     n = values.shape[0]
     part = n // (gys * levs)
     bits = levs.bit_length() - 1
-    copies = 2 + bits + (gys - 1) + 2 * (gys - 1) + 2 * bits + (levs - 1)
+    copies = 2 + PIPE * (bits + gys - 1) + 2 * (gys - 1) + 2 * bits + (levs - 1)
     vmem = pl.BlockSpec(memory_space=pltpu.VMEM)
     hbm = pl.BlockSpec(memory_space=pl.ANY)
     return pl.pallas_call(

time: 89.6 us -> 86.2 us (0.962)
  Pallas kernels: 79.2 us -> 75.8 us
    pallas_call x1, Pallas kernels: 73 us -> 69.6 us  [analysis_weights(): pl.pallas_call(functools.partial(analysis_weights_kernel, axes), name='an...]
where the time goes in v4:
time: 86.2 us; the launch traced here: 85.8 us
  Pallas kernels  75.8 us (88%)
  local copies, waits for them, and re-layouts  6.31 us (7%)
  other arithmetic  2.98 us (3%)
    pallas_call x1, Pallas kernels, analysis_weights(): pl.pallas_call(functools.partial(analysis_weights_kernel, axes), name='an...  69.6 us
    pallas_call x1, Pallas kernels, analyse(): pl.pallas_call(analyse_kernel, name='analyse', grid=(x_count // width,),...  6.18 us
    transpose x1, local copies, waits for them, and re-layouts, local(): state.transpose(1, 2, 0, 3).reshape(y_count * lev_count, x_count, members)  4.08 us

profile of v4, /device:TPU:0, one launch (start us, length us, event | category | flops | bytes accessed | tf_op | source)
XLA Modules:
  0.0 85.8 jit_solution(15805134791166127011)
XLA Ops:
  0.6 0.7 broadcast_compare_fusion.1
  1.3 0.7 broadcast_divide_fusion
  2.1 0.1 copy.38
  2.2 0.1 copy.39
  2.3 0.8 copy.30
  3.2 1.6 %select_select_fusion.code_ref = s32[512,8]{1,0:T(8,128)S(1)} fusion(s32[512,8]{1,0:T(8,128)S(1)} %copy.38, s32[512,8]{1,0:T(8,128)S(1)} %copy.39, s32[512,8]{1,0:T(8,128)S(1)} %copy.30, s32[512]{0:T(512)S(1)} %get-tuple-element.17, s32[512]{0:T(512)} %param.9, s32[]{:T(128)S(6)} %mul.16, s32[512]{0:T(512)} %param.10, ...), kind=kLoop, calls=%fused_computation.7 | loop fusion | flops 151552 | bytes 72708 | tf_op jit(solution)/shard_map/jit(_where)/select_n | solution.py:35
  4.7 0.0 copy-start.1
  4.8 0.0 copy-start.2
  4.8 4.1 %copy.41 = bf16[8,2,128,512]{3,2,1,0:T(8,128)(2,1)} copy(bf16[8,2,128,512]{3,1,0,2:T(2,128)(2,1)} %bitcast.15) | data formatting | bytes 4194304 | tf_op jit(solution)/shard_map/transpose | solution.py:449
  8.8 0.0 copy-start
  8.8 0.0 copy-done.1
  8.8 0.1 copy.42.val_ref
  9.0 0.0 copy-done.2
  9.0 0.1 copy.43.err_ref
  9.2 69.6 %analysis_weights.1 = (bf16[512,512]{1,0:T(8,128)(2,1)S(1)}, f32[512,128]{1,0:T(8,128)S(1)}, bf16[512,512]{1,0:T(8,128)(2,1)S(1)}, bf16[4,4,128,512]{3,2,1,0:T(8,128)(2,1)S(1)}) custom-call(s32[512,8]{1,0:T(8,128)S(1)} %select_select_fusion.code_ref, bf16[16,128,512]{2,1,0:T(8,128)(2,1)} %bitcast.14, f32[512,1]{1,0:T(8,128)S(1)} %copy.42.val_ref, ...), custom_call_target="tpu_custom_call" | custom-call | tf_op jit(solution)/shard_map/analysis_weights/pallas_call | solution.py:332
  78.8 0.1 slice_reduce_fusion
  78.9 0.0 copy-done
  79.0 6.2 %analyse.1 = (f32[128,128]{1,0:T(8,128)S(1)}, bf16[2048,512]{1,0:T(8,128)(2,1)}) custom-call(bf16[4,4,128,512]{3,2,1,0:T(8,128)(2,1)S(1)} %get-tuple-element.8.relaid_ref, bf16[2,128,512]{2,1,0:T(8,128)(2,1)S(1)} %bitcast.11, bf16[512,512]{1,0:T(8,128)(2,1)S(1)} %get-tuple-element.9.z_ref, bf16[512,512]{1,0:T(8,128)(2,1)S(1)} %get-tuple-element.10.y_ref, ...), custom_call_target="tpu_custom_call" | custom-call | tf_op jit(solution)/shard_map/analyse/pallas_call | solution.py:412
  85.2 0.7 copy.45
  (2 shorter events, 0.0 us)
Async XLA Ops:
  4.7 4.1 %copy-start.1 = (f32[512]{0:T(512)S(1)}, f32[512]{0:T(512)}, u32[]{:S(2)}) copy-start(f32[512]{0:T(512)} %param.13) | copy-start | bytes 6148
  4.8 4.2 %copy-start.2 = (f32[512]{0:T(512)S(1)}, f32[512]{0:T(512)}, u32[]{:S(2)}) copy-start(f32[512]{0:T(512)} %param.14) | copy-start | bytes 6148
  8.8 70.1 %copy-start = (bf16[128,2,512]{2,1,0:T(2,128)(2,1)S(1)}, bf16[128,2,512]{2,1,0:T(2,128)(2,1)}, u32[]{:S(2)}) copy-start(bf16[128,2,512]{2,1,0:T(2,128)(2,1)} %param.15) | copy-start | bytes 786436
